TPU v7x, 32 devices: a whole 2x2x4 slice. The times are simulated.
32 devices in a mesh: dp: 16 (over z, x, core), mp: 2 (over y).
Axes of the slice: x: 2, y: 2, z: 4, core: 2. Of those that a mesh axis runs over, the one named last changes fastest.
Arguments:
- inputs_store: bfloat16 [512, 128], replicated, may hold values from -6 to 6
- window: int32 [16], replicated, may hold values from 0 to 511
- targets_store: bfloat16 [512, 4096], P(None, ('dp', 'mp')), may hold values from -6 to 6
- jac_store: bfloat16 [512, 4096, 128], P(None, ('dp', 'mp')), may hold values from -4 to 4
- first_weight: bfloat16 [128, 1024], replicated, may hold values from -0.5 to 0.5
- first_bias: bfloat16 [1024], replicated, may hold values from -3 to 3
- hidden_weight: bfloat16 [1024, 1024], P(None, 'mp'), may hold values from -0.1875 to 0.1875
- hidden_bias: bfloat16 [1024], P('mp'), may hold values from -3 to 3
- decoder_weight: bfloat16 [4096, 1024], P(('dp', 'mp')), may hold values from -0.1875 to 0.1875
Outputs:
- first_weights: float32 [128, 1024], replicated
- first_biases: float32 [1024], replicated
- hidden_weights: float32 [1024, 1024], P(None, 'mp')
- hidden_biases: float32 [1024], P('mp')
- decoder_grad: float32 [4096, 1024], P(('dp', 'mp'))
Inputs may be any that keep to these rules, and one draw needn't show every extreme that they name: `window`: indices of stored samples; an index may repeat.
All inputs are finite; a program needn't handle non-finite values.
Results may differ from a plain program's by a relative error of at most 0.011.
Values may be sent and summed in bfloat16 or wider, within the bound.
A program may use at most 64 MiB of HBM per device.

v0:
```python
import jax
import jax.numpy as jnp
from jax import lax
from jax.sharding import PartitionSpec as P


def on_device(
    inputs_store,
    window,
    targets_store,
    jac_store,
    first_weight,
    first_bias,
    hidden_weight,
    hidden_bias,
    decoder_weight,
):
    each_count = window.shape[0] // lax.axis_size("dp")
    jac_window = jac_store[window]
    target_window = targets_store[window]
    jac_mine, target_mine = (
        lax.all_to_all(jac_window, "dp", split_axis=0, concat_axis=1, tiled=True),
        lax.all_to_all(target_window, "dp", split_axis=0, concat_axis=1, tiled=True),
    )
    mine_index = lax.dynamic_slice_in_dim(window, lax.axis_index("dp") * each_count, each_count)
    inputs = inputs_store[mine_index]
    weight_one = first_weight.astype(jnp.float32)
    first_pre = jnp.dot(
        inputs, first_weight, preferred_element_type=jnp.float32
    ) + first_bias.astype(jnp.float32)
    first_act = jnp.tanh(first_pre)
    first_slope = 1.0 - first_act * first_act
    first_tan = (first_slope[:, None, :] * weight_one[None]).astype(jnp.bfloat16)
    first_round = first_act.astype(jnp.bfloat16)
    hidden_lin = jnp.einsum(
        "srh,hk->srk", first_tan, hidden_weight, preferred_element_type=jnp.float32
    )
    hidden_pre = jnp.dot(
        first_round, hidden_weight, preferred_element_type=jnp.float32
    ) + hidden_bias.astype(jnp.float32)
    hidden_act = jnp.tanh(hidden_pre)
    hidden_slope = 1.0 - hidden_act * hidden_act
    hidden_tangent = (hidden_slope[:, None, :] * hidden_lin).astype(jnp.bfloat16)
    hidden_rounded_state = hidden_act.astype(jnp.bfloat16)
    act_all, tangent_full_rows = (
        lax.all_gather(hidden_rounded_state, "mp", axis=1, tiled=True),
        lax.all_gather(hidden_tangent, "mp", axis=2, tiled=True),
    )
    decoder_full_rows = lax.all_gather(decoder_weight, "dp", axis=0, tiled=True)
    outputs_net = jnp.einsum(
        "sk,ok->so", act_all, decoder_full_rows, preferred_element_type=jnp.float32
    )
    jacobian_predicted = jnp.einsum(
        "mvn,an->mav", tangent_full_rows, decoder_full_rows, preferred_element_type=jnp.float32
    )
    output_residual = (outputs_net - target_mine.astype(jnp.float32)).astype(jnp.bfloat16)
    jacobian_residual = (jacobian_predicted - jac_mine.astype(jnp.float32)).astype(jnp.bfloat16)
    decoder_grad = lax.psum_scatter(
        jnp.einsum("qi,qm->im", output_residual, act_all, preferred_element_type=jnp.float32)
        + jnp.einsum(
            "hzy,hym->zm", jacobian_residual, tangent_full_rows, preferred_element_type=jnp.float32
        ),
        "dp",
        scatter_dimension=0,
        tiled=True,
    )
    act_partial = jnp.einsum(
        "so,oh->sh", output_residual, decoder_full_rows, preferred_element_type=jnp.float32
    )
    tan_partial = jnp.einsum(
        "lud,uf->ldf", jacobian_residual, decoder_full_rows, preferred_element_type=jnp.float32
    )
    act_back, tan_back = (
        lax.psum_scatter(
            act_partial.astype(jnp.bfloat16), "mp", scatter_dimension=1, tiled=True
        ).astype(jnp.float32),
        lax.psum_scatter(
            tan_partial.astype(jnp.bfloat16), "mp", scatter_dimension=2, tiled=True
        ).astype(jnp.float32),
    )
    lin_back = tan_back * hidden_slope[:, None, :]
    pre_back = act_back * hidden_slope - 2.0 * hidden_act * hidden_slope * jnp.sum(
        tan_back * hidden_lin, axis=1
    )
    lin_round = lin_back.astype(jnp.bfloat16)
    pre_round = pre_back.astype(jnp.bfloat16)
    hidden_grad = jnp.einsum(
        "sh,sk->hk", first_round, pre_round, preferred_element_type=jnp.float32
    ) + jnp.einsum("srh,srk->hk", first_tan, lin_round, preferred_element_type=jnp.float32)
    hidden_bgrad = jnp.sum(pre_back, axis=0)
    tan_lower = jnp.einsum(
        "srk,hk->srh", lin_round, hidden_weight, preferred_element_type=jnp.float32
    )
    act_lower = jnp.einsum(
        "sk,hk->sh", pre_round, hidden_weight, preferred_element_type=jnp.float32
    )
    pre_lower = act_lower * first_slope - 2.0 * first_act * first_slope * jnp.sum(
        tan_lower * weight_one[None], axis=1
    )
    weight_part = jnp.einsum(
        "sr,sh->rh", inputs.astype(jnp.float32), pre_lower, precision=lax.Precision.HIGHEST
    ) + jnp.sum(tan_lower * first_slope[:, None, :], axis=0)
    bias_part = jnp.sum(pre_lower, axis=0)
    weight_mid, bias_mid = (
        lax.psum(weight_part.astype(jnp.bfloat16), "mp").astype(jnp.float32),
        lax.psum(bias_part.astype(jnp.bfloat16), "mp").astype(jnp.float32),
    )
    first_weights, first_biases, hidden_weights, hidden_biases = lax.psum(
        (weight_mid, bias_mid, hidden_grad, hidden_bgrad), "dp"
    )
    return (first_weights, first_biases, hidden_weights, hidden_biases, decoder_grad)


def solution(mesh):
    placed = (
        P(),
        P(),
        P(None, ("dp", "mp")),
        P(None, ("dp", "mp"), None),
        P(),
        P(),
        P(None, "mp"),
        P("mp"),
        P(("dp", "mp"), None),
    )
    return jax.shard_map(
        on_device,
        mesh=mesh,
        in_specs=placed,
        out_specs=(P(), P(), P(None, "mp"), P("mp"), P(("dp", "mp"), None)),
        check_vma=False,
    )
```

profile of v0, /device:TPU:0, one launch (start us, length us, event | category | flops | bytes accessed | tf_op | source)
XLA Modules:
  0.0 348.1 jit_solution(14651161969415206212)
XLA Ops:
  8.6 1.5 gather_fusion
  10.7 7.4 %all-to-all-start = ((bf16[16,1,128]{2,1,0:T(2,128)(2,1)}), bf16[16,1,128]{2,1,0:T(2,128)(2,1)S(1)}, u32[]{:S(2)}, u32[]{:S(2)}) async-start(bf16[16,1,128]{2,1,0:T(2,128)(2,1)} %copy.16), calls=%async_computation | async-start | bytes 16384 | tf_op jit(solution)/shard_map/all_to_all | solution.py:23
  18.1 1.2 dynamic_slice.3
  21.3 1.1 fusion.18
  22.4 7.2 %gather_fusion.1 = bf16[16,128,128]{2,1,0:T(8,128)(2,1)} fusion(bf16[512,128,128]{2,1,0:T(8,128)(2,1)} %param.12, s32[1024]{0:T(1024)S(1)} %pad_clamp_fusion), kind=kCustom, calls=%fused_computation.1 | custom fusion | bytes 1048640 | tf_op jit(solution)/shard_map/gather | solution.py:19
  29.6 6.0 %all-to-all-start.1 = ((bf16[16,128,128]{2,1,0:T(8,128)(2,1)}), bf16[16,128,128]{2,1,0:T(8,128)(2,1)S(1)}, u32[]{:S(2)}, u32[]{:S(2)}) async-start(bf16[16,128,128]{2,1,0:T(8,128)(2,1)} %gather_fusion.1), calls=%async_computation.1 | async-start | bytes 1048576 | tf_op jit(solution)/shard_map/all_to_all | solution.py:22
  35.7 0.7 fusion.22
  36.6 0.7 fusion.20
  37.3 4.4 %all-gather.2 = bf16[2,1,512]{2,1,0:T(2,128)(2,1)S(1)} all-gather(bf16[1,1,512]{2,1,0:T(2,128)(2,1)S(1)} %reshape.173), channel_id=2, replica_groups=mesh['dp'=16,'mp'=2] {'mp'}, dimensions={0}, use_global_device_ids=true | all-gather | bytes 3072 | tf_op jit(solution)/shard_map/all_gather | solution.py:46
  41.7 2.0 multiply_convert_fusion
  43.7 5.6 %all-gather.1 = bf16[128,1024]{1,0:T(8,128)(2,1)S(1)} all-gather(bf16[128,512]{1,0:T(8,128)(2,1)S(1)} %get-tuple-element.30), channel_id=3, replica_groups=mesh['dp'=16,'mp'=2] {'mp'}, dimensions={1}, use_global_device_ids=true | all-gather | bytes 393216 | tf_op jit(solution)/shard_map/all_gather | solution.py:47
  49.3 6.6 %all-to-all-done.1 = bf16[16,128,128]{2,1,0:T(8,128)(2,1)S(1)} async-done(((bf16[16,128,128]{2,1,0:T(8,128)(2,1)}), bf16[16,128,128]{2,1,0:T(8,128)(2,1)S(1)}, u32[]{:S(2)}, u32[]{:S(2)}) %all-to-all-start.1) | async-done | bytes 524320 | tf_op jit(solution)/shard_map/all_to_all | solution.py:22
  56.4 13.1 %all-gather.5.cloned.1.call-done = bf16[2048,1024]{1,0:T(8,128)(2,1)} async-done(((bf16[128,1024]{1,0:T(8,128)(2,1)}), bf16[2048,1024]{1,0:T(8,128)(2,1)}) %all-gather.5.cloned.1.call-update) | async-done | bytes 4194320 | tf_op jit(solution)/shard_map/all_gather | solution.py:49
  69.4 3.5 %fusion.26 = f32[1,2048]{1,0:T(1,128)S(1)} fusion(bf16[1024,1]{0,1:T(2,128)(2,1)S(1)} %bitcast.62, bf16[2048,1024]{1,0:T(8,128)(2,1)} %all-gather.5.cloned.1.call-done), kind=kOutput, calls=%fused_computation.48 | convolution fusion | flops 4194304 | bytes 4204544 | tf_op jit(solution)/shard_map/sk,ok->so/dot_general | solution.py:50
  73.6 0.9 reshape_bitcast_fusion
  74.6 3.8 %fusion.1 = bf16[2048,128]{0,1:T(8,128)(2,1)S(1)} fusion(f32[2048,128]{0,1:T(8,128)S(1)} %copy.18, bf16[128,1024]{1,0:T(8,128)(2,1)S(1)} %all-gather.1, bf16[2048,1024]{1,0:T(8,128)(2,1)} %all-gather.5.cloned.1.call-done), kind=kOutput, calls=%fused_computation.5 | convolution fusion | flops 537395200 | bytes 6029312 | tf_op jit(solution)/shard_map/mvn,an->mav/dot_general | solution.py:53
  78.6 1.4 fusion.2
  80.1 0.7 bitcast_convert_fusion.1
  80.8 4.4 %reduce-scatter.10.cloned.1.call-done = bf16[512,1]{1,0:T(8,128)(2,1)} async-done(((bf16[1024,1]{1,0:T(8,128)(2,1)}), bf16[512,1]{1,0:T(8,128)(2,1)}) %reduce-scatter.10.cloned.1.call-update) | async-done | bytes 1040
  85.2 1.0 copy.20
  86.2 13.6 %reduce-scatter.6.cloned.1.call-done = bf16[1,128,512]{2,1,0:T(8,128)(2,1)} async-done(((bf16[1,128,1024]{2,1,0:T(8,128)(2,1)}), bf16[1,128,512]{2,1,0:T(8,128)(2,1)}) %reduce-scatter.6.cloned.1.call-update) | async-done | bytes 131088 | tf_op jit(solution)/shard_map/reduce_scatter | solution.py:77
  99.9 1.0 fusion.5
  101.3 1.4 fusion.4
  102.7 0.8 add_convert_fusion
  103.7 1.8 multiply_add_fusion.1
  105.6 4.5 %multiply_add_fusion = f32[2048,1024]{1,0:T(8,128)} fusion(bf16[2048,128]{0,1:T(8,128)(2,1)S(1)} %fusion.1, bf16[128,1024]{1,0:T(8,128)(2,1)S(1)} %all-gather.1, f32[1024]{0:T(1024)S(1)} %convert.21, f32[2048]{0:T(1024)S(1)} %get-tuple-element.19), kind=kOutput, calls=%fused_computation.2 | convolution fusion | flops 541065216 | bytes 9187328 | tf_op jit(solution)/shard_map/hzy,hym->zm/dot_general | solution.py:60
  110.1 4.9 %psum.44 = bf16[1024]{0:T(1024)(128)(2,1)S(1)} all-reduce(bf16[1024]{0:T(1024)(128)(2,1)S(1)} %get-tuple-element.25), channel_id=1, replica_groups=mesh['dp'=16,'mp'=2] {'mp'}, use_global_device_ids=true, to_apply=%region_6.0 | all-reduce | flops 1024 | bytes 4096 | tf_op jit(solution)/shard_map/psum | solution.py:106
  115.1 12.0 %all-reduce.5.cloned.1.call-done = bf16[128,1024]{1,0:T(8,128)(2,1)} async-done(((bf16[128,1024]{1,0:T(8,128)(2,1)}), bf16[128,1024]{1,0:T(8,128)(2,1)}) %all-reduce.5.cloned.1.call-update) | async-done | bytes 262160 | tf_op jit(solution)/shard_map/psum | solution.py:105
  127.1 70.9 %all-reduce.8 = (f32[128,1024]{1,0:T(8,128)}, f32[1024]{0:T(1024)}, f32[512]{0:T(512)}) all-reduce(bf16[128,1024]{1,0:T(8,128)(2,1)} %all-reduce.5.cloned.1.call-done, bf16[1024]{0:T(1024)(128)(2,1)S(1)} %psum.44, f32[512]{0:T(512)S(1)} %bitcast.67), channel_id=1, replica_groups=mesh['dp'=16,'mp'=2] {'dp'}, use_global_device_ids=true, to_apply=%region_5.0 | all-reduce | flops 132608 | bytes 796672 | tf_op jit(solution)/shard_map/psum | solution.py:108
  198.0 33.0 %all-reduce.7.cloned.1.call-done = f32[1024,512]{1,0:T(8,128)} async-done(((f32[1024,512]{1,0:T(8,128)}), f32[1024,512]{1,0:T(8,128)}) %all-reduce.7.cloned.1.call-update) | async-done | bytes 2097168 | tf_op jit(solution)/shard_map/psum | solution.py:108
  231.0 107.3 %reduce-scatter.8.cloned.1.call-done = f32[128,1024]{1,0:T(8,128)} async-done(((f32[2048,1024]{1,0:T(8,128)}), f32[128,1024]{1,0:T(8,128)}) %reduce-scatter.8.cloned.1.call-update) | async-done | bytes 524304 | tf_op jit(solution)/shard_map/reduce_scatter | solution.py:58
  338.2 3.1 copy.29
  (50 shorter events, 4.2 us)
Async XLA Ops:
  7.2 29.2 %copy-start = (bf16[1024,512]{1,0:T(8,128)(2,1)S(1)}, bf16[1024,512]{1,0:T(8,128)(2,1)}, u32[]{:S(2)}) copy-start(bf16[1024,512]{1,0:T(8,128)(2,1)} %param.15) | copy-start | bytes 3145732
  7.2 62.2 %all-gather.5.cloned.1.call-start = ((), (), s32[]{:S(2)}) async-start(), calls=%async_computation.5 | async-start | bytes 4456448 | tf_op jit(solution)/shard_map/all_gather | solution.py:49
  10.7 18.9 %all-to-all-start = ((bf16[16,1,128]{2,1,0:T(2,128)(2,1)}), bf16[16,1,128]{2,1,0:T(2,128)(2,1)S(1)}, u32[]{:S(2)}, u32[]{:S(2)}) async-start(bf16[16,1,128]{2,1,0:T(2,128)(2,1)} %copy.16), calls=%async_computation | async-start | bytes 16384 | tf_op jit(solution)/shard_map/all_to_all | solution.py:23
  29.6 26.3 %all-to-all-start.1 = ((bf16[16,128,128]{2,1,0:T(8,128)(2,1)}), bf16[16,128,128]{2,1,0:T(8,128)(2,1)S(1)}, u32[]{:S(2)}, u32[]{:S(2)}) async-start(bf16[16,128,128]{2,1,0:T(8,128)(2,1)} %gather_fusion.1), calls=%async_computation.1 | async-start | bytes 1048576 | tf_op jit(solution)/shard_map/all_to_all | solution.py:22
  35.6 49.6 %reduce-scatter.10.cloned.1.call-start = ((), (), s32[]{:S(2)}) async-start(), calls=%async_computation.10 | async-start | bytes 393216
  69.4 3.6 %copy-start.1 = (bf16[2048,1024]{1,0:T(8,128)(2,1)S(1)}, bf16[2048,1024]{1,0:T(8,128)(2,1)}, u32[]{:S(2)}) copy-start(bf16[2048,1024]{1,0:T(8,128)(2,1)} %all-gather.5.cloned.1.call-done) | copy-start | bytes 12582916
  74.6 25.3 %reduce-scatter.6.cloned.1.call-start = ((), (), s32[]{:S(2)}) async-start(), calls=%async_computation.6 | async-start | bytes 393216 | tf_op jit(solution)/shard_map/reduce_scatter | solution.py:77
  74.6 3.9 %copy-start.2 = (bf16[2048,1024]{1,0:T(8,128)(2,1)S(1)}, bf16[2048,1024]{1,0:T(8,128)(2,1)}, u32[]{:S(2)}) copy-start(bf16[2048,1024]{1,0:T(8,128)(2,1)} %all-gather.5.cloned.1.call-done) | copy-start | bytes 12582916
  78.5 21.4 %copy-start.5 = (f32[128,512]{1,0:T(8,128)S(1)}, f32[128,512]{1,0:T(8,128)}, u32[]{:S(2)}) copy-start(f32[128,512]{1,0:T(8,128)} %get-tuple-element.31) | copy-start | bytes 786436
  78.5 22.4 %copy-start.7 = (bf16[512]{0:T(512)(128)(2,1)S(1)}, bf16[512]{0:T(512)(128)(2,1)}, u32[]{:S(2)}) copy-start(bf16[512]{0:T(512)(128)(2,1)} %param.16) | copy-start | bytes 3076
  78.5 22.8 %copy-start.3 = (bf16[128,1024]{1,0:T(8,128)(2,1)S(1)}, bf16[128,1024]{1,0:T(8,128)(2,1)}, u32[]{:S(2)}) copy-start(bf16[128,1024]{1,0:T(8,128)(2,1)} %param.13) | copy-start | bytes 786436
  78.5 24.2 %copy-start.6 = (bf16[1024]{0:T(1024)(128)(2,1)S(1)}, bf16[1024]{0:T(1024)(128)(2,1)}, u32[]{:S(2)}) copy-start(bf16[1024]{0:T(1024)(128)(2,1)} %param.14) | copy-start | bytes 6148
  80.0 47.1 %all-reduce.5.cloned.1.call-start = ((), (), s32[]{:S(2)}) async-start(), calls=%async_computation.7 | async-start | bytes 524288 | tf_op jit(solution)/shard_map/psum | solution.py:105
  99.9 3.8 %copy-start.4 = (bf16[1,128,512]{2,1,0:T(8,128)(2,1)S(1)}, bf16[1,128,512]{2,1,0:T(8,128)(2,1)}, u32[]{:S(2)}) copy-start(bf16[1,128,512]{2,1,0:T(8,128)(2,1)} %reduce-scatter.6.cloned.1.call-done) | copy-start | bytes 393220
  103.6 127.4 %all-reduce.7.cloned.1.call-start = ((), (), s32[]{:S(2)}) async-start(), calls=%async_computation.8 | async-start | bytes 4194304 | tf_op jit(solution)/shard_map/psum | solution.py:108
  105.5 232.7 %reduce-scatter.8.cloned.1.call-start = ((), (), s32[]{:S(2)}) async-start(), calls=%async_computation.9 | async-start | bytes 8912896 | tf_op jit(solution)/shard_map/reduce_scatter | solution.py:58
Sparse Core Ops, SparseCore 0:
  10.1 59.2 all-gather.4
  74.7 10.4 reduce-scatter.9
  88.0 11.7 reduce-scatter.5
  103.7 23.3 all-reduce.4
  131.1 99.8 all-reduce.6
  235.4 102.7 reduce-scatter.7
where the time goes:
time: 349 us; the launch traced here: 348 us
  waiting for transfers between devices  191 us (55%)
  blocking collectives  85.8 us (25%)
  matrix products  20.9 us (6%)
  between operations  16.3 us (5%)
  local copies, waits for them, and re-layouts  16 us (5%)
  starting transfers between devices  13.6 us (4%)
  other arithmetic  4.8 us (1%)
    reduce_scatter x1, waiting for transfers between devices, on_device(): lax.psum_scatter(jnp.einsum('qi,qm->im', output_residual, act_all, prefer...  107 us
    psum x1, blocking collectives, on_device(): lax.psum((weight_mid, bias_mid, hidden_grad, hidden_bgrad), 'dp')  70.9 us
    psum x1, waiting for transfers between devices, on_device(): lax.psum((weight_mid, bias_mid, hidden_grad, hidden_bgrad), 'dp')  33 us
    reduce_scatter x1, waiting for transfers between devices, on_device(): lax.psum_scatter(tan_partial.astype(jnp.bfloat16), 'mp', scatter_dimensio...  13.6 us
    all_gather x1, waiting for transfers between devices, on_device(): decoder_full_rows = lax.all_gather(decoder_weight, 'dp', axis=0, tiled=True)  13.1 us
    psum x1, waiting for transfers between devices, on_device(): lax.psum(weight_part.astype(jnp.bfloat16), 'mp').astype(jnp.float32)  12 us
    all_to_all x1, starting transfers between devices, on_device(): lax.all_to_all(target_window, 'dp', split_axis=0, concat_axis=1, tiled=True)  7.39 us
    gather x1, local copies, waits for them, and re-layouts, on_device(): jac_window = jac_store[window]  7.22 us
  transfers between devices with their start and end apart: 8, of which 7 were waited for; matrix products, arithmetic and copies ran while one was open for 9% of the time, Pallas kernels for 0%

commit v1 on v0

v1 whole, which is shorter than its diff:
```python
import jax
import jax.numpy as jnp
from jax import lax
from jax.sharding import PartitionSpec as P

F32 = jnp.float32
BF16 = jnp.bfloat16


def dot(spec, a, b):
    return jnp.einsum(spec, a, b, preferred_element_type=F32)


def on_device(
    inputs_store,
    window,
    targets_store,
    jac_store,
    first_weight,
    first_bias,
    hidden_weight,
    hidden_bias,
    decoder_weight,
):
    dp, mp = lax.axis_size("dp"), lax.axis_size("mp")
    at = lax.axis_index("dp")
    samples = window.shape[0]
    each = samples // dp
    rank, hidden = first_weight.shape
    own_hidden = hidden_weight.shape[1]
    out_rows = decoder_weight.shape[0]

    share = hidden // dp
    pad = 16
    piece = jnp.concatenate(
        [
            lax.dynamic_slice_in_dim(hidden_weight, at * share, share),
            jnp.broadcast_to(hidden_bias[None], (pad, own_hidden)),
        ],
        axis=0,
    )
    pieces = lax.all_gather(piece, ("dp", "mp"), axis=0).reshape(dp, mp, share + pad, own_hidden)
    weight_two = pieces[:, :, :share].transpose(0, 2, 1, 3).reshape(hidden, mp * own_hidden)
    bias_two = pieces[0, :, share].reshape(mp * own_hidden).astype(F32)

    decoder_group = lax.all_gather(decoder_weight, "dp", axis=0)

    inputs = inputs_store[window]
    weight_one = first_weight.astype(F32)
    first_act = jnp.tanh(dot("sr,rh->sh", inputs, first_weight) + first_bias.astype(F32))
    first_slope = 1.0 - first_act * first_act
    first_tan = (first_slope[:, None, :] * weight_one[None]).astype(BF16)
    first_round = first_act.astype(BF16)

    hidden_act = jnp.tanh(dot("sh,hk->sk", first_round, weight_two) + bias_two)
    hidden_slope = 1.0 - hidden_act * hidden_act
    hidden_tan = (hidden_slope[:, None, :] * dot("srh,hk->srk", first_tan, weight_two)).astype(BF16)
    hidden_round = hidden_act.astype(BF16)

    targets = targets_store[window].astype(F32)
    jacobians = jac_store[window].astype(F32)
    out_miss = (dot("sk,ok->so", hidden_round, decoder_weight) - targets).astype(BF16)
    jac_miss = (dot("srk,ok->sor", hidden_tan, decoder_weight) - jacobians).astype(BF16)

    extra = -(-out_rows // rank)
    rider = jnp.pad(out_miss, ((0, 0), (0, extra * rank - out_rows))).reshape(samples, extra, rank)
    packed = jnp.concatenate([jac_miss, rider], axis=1).reshape(dp, each, out_rows + extra, rank)
    mine = lax.all_to_all(packed, "dp", split_axis=0, concat_axis=0, tiled=True)

    decoder_grad = dot("so,sk->ok", out_miss, hidden_round) + dot(
        "sor,srk->ok", jac_miss, hidden_tan
    )

    out_mine = mine[:, :, out_rows:].reshape(dp, each, extra * rank)[:, :, :out_rows]
    tan_part = dot("pcor,pok->crk", mine[:, :, :out_rows], decoder_group).astype(BF16)
    act_part = dot("pco,pok->ck", out_mine, decoder_group).astype(BF16)
    part = jnp.concatenate([tan_part, act_part[:, None]], axis=1)
    part = part.reshape(each, rank + 1, mp, own_hidden).transpose(2, 0, 1, 3)
    back = jnp.sum(
        lax.all_to_all(part, "mp", split_axis=0, concat_axis=0, tiled=True).astype(F32), axis=0
    )
    tan_back, act_back = back[:, :rank], back[:, rank]

    tan_own = lax.dynamic_slice_in_dim(first_tan, at * each, each)
    round_own = lax.dynamic_slice_in_dim(first_round, at * each, each)
    lin_own = dot("srh,hk->srk", tan_own, hidden_weight)
    act_own = jnp.tanh(dot("sh,hk->sk", round_own, hidden_weight) + hidden_bias.astype(F32))
    slope_own = 1.0 - act_own * act_own
    lin_back = tan_back * slope_own[:, None, :]
    pre_back = act_back * slope_own - 2.0 * act_own * slope_own * jnp.sum(tan_back * lin_own, axis=1)
    send = jnp.concatenate([lin_back, pre_back[:, None]], axis=1).astype(BF16)

    full = lax.all_gather(send, "dp", axis=0, tiled=True)
    lin_round, pre_round = full[:, :rank], full[:, rank]
    hidden_weights = dot("sh,sk->hk", first_round, pre_round) + dot(
        "srh,srk->hk", first_tan, lin_round
    )
    hidden_biases = jnp.sum(pre_round.astype(F32), axis=0)
    tan_lower = dot("srk,hk->srh", lin_round, hidden_weight)
    act_lower = dot("sk,hk->sh", pre_round, hidden_weight)
    pre_lower = act_lower * first_slope - 2.0 * first_act * first_slope * jnp.sum(
        tan_lower * weight_one[None], axis=1
    )
    weight_part = jnp.einsum(
        "sr,sh->rh", inputs.astype(F32), pre_lower, precision=lax.Precision.HIGHEST
    ) + jnp.sum(tan_lower * first_slope[:, None, :], axis=0)
    bias_part = jnp.sum(pre_lower, axis=0)
    both = jnp.concatenate([weight_part, bias_part[None]], axis=0).astype(BF16)
    total = jnp.sum(lax.all_gather(both, "mp", axis=0).astype(F32), axis=0)
    return total[:rank], total[rank], hidden_weights, hidden_biases, decoder_grad


def solution(mesh):
    placed = (
        P(),
        P(),
        P(None, ("dp", "mp")),
        P(None, ("dp", "mp"), None),
        P(),
        P(),
        P(None, "mp"),
        P("mp"),
        P(("dp", "mp"), None),
    )
    return jax.shard_map(
        on_device,
        mesh=mesh,
        in_specs=placed,
        out_specs=(P(), P(), P(None, "mp"), P("mp"), P(("dp", "mp"), None)),
        check_vma=False,
    )
```

time: 349 us -> 221 us (0.63)
  blocking collectives: 85.8 us -> 9.46 us
  waiting for transfers between devices: 191 us -> 120 us
  matrix products: 20.9 us -> 32.5 us
  local copies, waits for them, and re-layouts: 16 us -> 25.2 us
  other arithmetic: 4.8 us -> 10.6 us
  starting transfers between devices: 13.6 us -> 8.03 us
    reduce_scatter x2 -> x0, waiting for transfers between devices: 121 us -> none  [the longest x1 107 us: on_device(): lax.psum_scatter(jnp.einsum('qi,qm->im', output_residual, act_all, prefer...]
    all_gather x1 -> x3, waiting for transfers between devices: 13.1 us -> 93.3 us  [the longest x1 46.5 us: on_device(): lax.all_gather(piece, ('dp', 'mp'), axis=0)]
    psum x2 -> x0, blocking collectives: 75.8 us -> none  [the longest x1 70.9 us: on_device(): lax.psum((weight_mid, bias_mid, hidden_grad, hidden_bgrad), 'dp')]
    psum x2 -> x0, waiting for transfers between devices: 45 us -> none  [the longest x1 33 us: on_device(): lax.psum((weight_mid, bias_mid, hidden_grad, hidden_bgrad), 'dp')]
    all_to_all x2, waiting for transfers between devices: 6.61 us -> 26.4 us  [the longest x1 20.9 us: on_device(): mine = lax.all_to_all(packed, 'dp', split_axis=0, concat_axis=0, tiled=True)]
    dot_general x11 -> x16, matrix products: 20.9 us -> 32.5 us  [the longest x15 32.1 us: dot(): return jnp.einsum(spec, a, b, preferred_element_type=F32)]
    all_to_all x2, starting transfers between devices: 13.4 us -> 7.72 us  [the longest x1 4.28 us: on_device(): mine = lax.all_to_all(packed, 'dp', split_axis=0, concat_axis=0, tiled=True)]
    convert_element_type x7 -> x5, other arithmetic: 1.67 us -> 6.23 us  [the longest x1 3.03 us: on_device(): first_tan = (first_slope[:, None, :] * weight_one[None]).astype(BF16)]
  transfers between devices with their start and end apart: 8 -> 5, of which waited for: 7 -> 5; matrix products, arithmetic and copies ran while one was open for 9% -> 19% of each run, Pallas kernels for 0% -> 0%
where the time goes in v1:
time: 221 us; the launch traced here: 220 us
  waiting for transfers between devices  120 us (54%)
  matrix products  32.5 us (15%)
  local copies, waits for them, and re-layouts  25.2 us (11%)
  between operations  14 us (6%)
  other arithmetic  10.6 us (5%)
  blocking collectives  9.46 us (4%)
  starting transfers between devices  8.03 us (4%)
    all_gather x1, waiting for transfers between devices, on_device(): lax.all_gather(piece, ('dp', 'mp'), axis=0)  46.5 us
    all_gather x1, waiting for transfers between devices, on_device(): full = lax.all_gather(send, 'dp', axis=0, tiled=True)  36.2 us
    dot_general x15, matrix products, dot(): return jnp.einsum(spec, a, b, preferred_element_type=F32)  32.1 us
    all_to_all x1, waiting for transfers between devices, on_device(): mine = lax.all_to_all(packed, 'dp', split_axis=0, concat_axis=0, tiled=True)  20.9 us
    all_gather x1, waiting for transfers between devices, on_device(): decoder_group = lax.all_gather(decoder_weight, 'dp', axis=0)  10.6 us
    all_gather x1, blocking collectives, on_device(): total = jnp.sum(lax.all_gather(both, 'mp', axis=0).astype(F32), axis=0)  9.46 us
    gather x1, local copies, waits for them, and re-layouts, on_device(): jacobians = jac_store[window].astype(F32)  7.17 us
    all_to_all x1, waiting for transfers between devices, on_device(): lax.all_to_all(part, 'mp', split_axis=0, concat_axis=0, tiled=True)  5.54 us
  transfers between devices with their start and end apart: 5, of which 5 were waited for; matrix products, arithmetic and copies ran while one was open for 19% of the time, Pallas kernels for 0%

profile of v1, /device:TPU:0, one launch (start us, length us, event | category | flops | bytes accessed | tf_op | source)
XLA Modules:
  0.0 220.3 jit_solution(12952913413949428980)
XLA Ops:
  7.2 1.2 copy-done
  11.2 1.8 convert_element_type.82
  13.6 1.5 gather_fusion
  15.1 7.2 %gather_fusion.1 = bf16[16,128,128]{2,1,0:T(8,128)(2,1)} fusion(bf16[512,128,128]{2,1,0:T(8,128)(2,1)} %param.12, s32[1024]{0:T(1024)S(1)} %pad_clamp_fusion), kind=kCustom, calls=%fused_computation.1 | custom fusion | bytes 1048640 | tf_op jit(solution)/shard_map/gather | solution.py:61
  22.3 1.5 gather_fusion.2
  23.8 1.7 fusion.28
  25.5 46.5 %all-gather.8.cloned.1.call-done = bf16[2560,512]{1,0:T(8,128)(2,1)} async-done(((bf16[80,512]{1,0:T(8,128)(2,1)}), bf16[2560,512]{1,0:T(8,128)(2,1)}) %all-gather.8.cloned.1.call-update) | async-done | bytes 2621456 | tf_op jit(solution)/shard_map/all_gather | solution.py:42
  72.0 1.8 slice.46
  73.8 2.2 copy.58
  76.0 1.9 copy.44
  77.9 2.7 %reshape.183 = bf16[1024,1024,1]{1,0,2:T(8,128)(2,1)} reshape(bf16[16,64,2,512]{3,2,1,0:T(2,128)(2,1)S(1)} %bitcast.95) | data formatting | bytes 4194304 | tf_op jit(solution)/shard_map/reshape | solution.py:43
  81.4 2.0 multiply_subtract_fusion.1
  83.6 6.5 %multiply_convert_fusion = bf16[16,128,1024]{2,1,0:T(8,128)(2,1)S(1)} fusion(f32[16,1024]{1,0:T(8,128)S(1)} %get-tuple-element.14, bf16[1024,1024,1]{1,0,2:T(8,128)(2,1)} %reshape.183, f32[128,1024]{1,0:T(8,128)} %convert_element_type.82, f32[16,1024]{1,0:T(8,128)S(1)} %get-tuple-element.10), kind=kOutput, calls=%fused_computation.5 | convolution fusion | flops 4303355904 | bytes 6946816 | tf_op jit(solution)/shard_map/srh,hk->srk/dot_general | solution.py:11
  90.1 2.0 copy-done.1
  92.0 1.5 fusion.5
  94.4 4.3 %all-to-all-start = ((bf16[16,1,129,128]{3,2,1,0:T(8,128)(2,1)}), bf16[16,1,129,128]{3,2,1,0:T(8,128)(2,1)S(1)}, u32[]{:S(2)}, u32[]{:S(2)}) async-start(bf16[16,1,129,128]{3,2,1,0:T(8,128)(2,1)} %maximum_bitcast_fusion), calls=%async_computation | async-start | bytes 1114112 | tf_op jit(solution)/shard_map/all_to_all | solution.py:68
  98.7 3.0 %multiply_convert_fusion.1 = bf16[16,128,1024]{2,1,0:T(8,128)(2,1)} fusion(f32[128,1024]{1,0:T(8,128)S(1)} %copy-done.3, f32[16,1024]{1,0:T(8,128)S(1)} %get-tuple-element.10), kind=kLoop, calls=%fused_computation.6 | loop fusion | flops 4194304 | bytes 4784128 | tf_op jit(solution)/shard_map/convert_element_type | solution.py:52
  101.7 20.9 %all-to-all-done = bf16[16,1,129,128]{3,2,1,0:T(8,128)(2,1)S(1)} async-done(((bf16[16,1,129,128]{3,2,1,0:T(8,128)(2,1)}), bf16[16,1,129,128]{3,2,1,0:T(8,128)(2,1)S(1)}, u32[]{:S(2)}, u32[]{:S(2)}) %all-to-all-start) | async-done | bytes 528416 | tf_op jit(solution)/shard_map/all_to_all | solution.py:68
  122.6 10.6 %all-gather.10.cloned.1.call-done = bf16[2048,1024]{1,0:T(8,128)(2,1)} async-done(((bf16[128,1024]{1,0:T(8,128)(2,1)}), bf16[2048,1024]{1,0:T(8,128)(2,1)}) %all-gather.10.cloned.1.call-update) | async-done | bytes 4194320 | tf_op jit(solution)/shard_map/all_gather | solution.py:46
  133.2 2.9 %fusion.6 = bf16[128,1024]{1,0:T(8,128)(2,1)S(1)} fusion(bf16[16,128,1024]{2,1,0:T(8,128)(2,1)} %bitcast.96, bf16[16,1,129,128]{3,2,1,0:T(8,128)(2,1)S(1)} %all-to-all-done), kind=kOutput, calls=%fused_computation.19 | convolution fusion | flops 537001984 | bytes 4980736 | tf_op jit(solution)/shard_map/pcor,pok->crk/dot_general | solution.py:11
  136.4 2.8 %fusion.21 = f32[1,1024,1]{1,0,2:T(1,128)S(1)} fusion(bf16[16,128,1024]{2,1,0:T(8,128)(2,1)} %bitcast.97, bf16[16,128,1]{1,0,2:T(8,128)(2,1)S(1)} %bitcast.105), kind=kOutput, calls=%fused_computation.52 | convolution fusion | flops 4194304 | bytes 4202496 | tf_op jit(solution)/shard_map/pco,pok->ck/dot_general | solution.py:11
  140.0 3.4 %all-to-all-start.1 = ((bf16[2,1,129,512]{3,2,1,0:T(8,128)(2,1)}), bf16[2,1,129,512]{3,2,1,0:T(8,128)(2,1)S(1)}, u32[]{:S(2)}, u32[]{:S(2)}) async-start(bf16[2,1,129,512]{3,2,1,0:T(8,128)(2,1)} %maximum_bitcast_fusion.1), calls=%async_computation.1 | async-start | bytes 557056 | tf_op jit(solution)/shard_map/all_to_all | solution.py:80
  143.9 5.5 %all-to-all-done.1 = bf16[2,1,129,512]{3,2,1,0:T(8,128)(2,1)S(1)} async-done(((bf16[2,1,129,512]{3,2,1,0:T(8,128)(2,1)}), bf16[2,1,129,512]{3,2,1,0:T(8,128)(2,1)S(1)}, u32[]{:S(2)}, u32[]{:S(2)}) %all-to-all-start.1) | async-done | bytes 264224 | tf_op jit(solution)/shard_map/all_to_all | solution.py:80
  149.5 1.3 fusion.10
  151.6 2.9 %convolution_bitcast_fusion.1 = f32[128,1024]{1,0:T(8,128)S(1)} fusion(bf16[16,128,128]{2,1,0:T(8,128)(2,1)S(1)} %fusion.5, bf16[16,128,1024]{2,1,0:T(8,128)(2,1)} %copy-done.1), kind=kOutput, calls=%fused_computation.17 | convolution fusion | flops 536870912 | bytes 5242880 | tf_op jit(solution)/shard_map/sor,srk->ok/dot_general | solution.py:11
  154.5 1.0 convolution_add_fusion
  155.5 36.2 %all-gather.6.cloned.1.call-done = bf16[16,129,512]{2,1,0:T(8,128)(2,1)} async-done(((bf16[1,129,512]{2,1,0:T(8,128)(2,1)}), bf16[16,129,512]{2,1,0:T(8,128)(2,1)}) %all-gather.6.cloned.1.call-update) | async-done | bytes 2113552 | tf_op jit(solution)/shard_map/all_gather | solution.py:93
  191.7 0.9 slice.52
  192.7 4.5 %multiply_reduce_fusion = (f32[128,1024]{1,0:T(8,128)S(1)}, f32[16,1024]{1,0:T(8,128)S(1)}) fusion(f32[16,1024]{1,0:T(8,128)S(1)} %get-tuple-element.10, f32[128,1024]{1,0:T(8,128)S(1)} %copy-done.3, bf16[1024,512]{1,0:T(8,128)(2,1)S(1)} %copy-done, bf16[16,129,512]{2,1,0:T(8,128)(2,1)} %all-gather.6.cloned.1.call-done), kind=kOutput, calls=%fused_computation.3 | convolution fusion | flops 2155724800 | bytes 4325376 | tf_op jit(solution)/shard_map/srk,hk->srh/dot_general | solution.py:11
  198.0 9.5 %all_gather.24 = bf16[2,129,1024]{2,1,0:T(8,128)(2,1)S(1)} all-gather(bf16[1,129,1024]{2,1,0:T(8,128)(2,1)S(1)} %pad_maximum_fusion), channel_id=1, replica_groups=mesh['dp'=16,'mp'=2] {'mp'}, dimensions={0}, use_global_device_ids=true | all-gather | bytes 792576 | tf_op jit(solution)/shard_map/all_gather | solution.py:109
  209.6 2.4 %fusion = f32[1024,512,1]{1,0,2:T(8,128)S(1)} fusion(bf16[16,129,512]{2,1,0:T(8,128)(2,1)S(1)} %copy-done.7, f32[128,1024]{1,0:T(8,128)S(1)} %copy-done.3, f32[16,1024]{1,0:T(8,128)S(1)} %get-tuple-element.10), kind=kOutput, calls=%fused_computation.8 | convolution fusion | flops 2151677952 | bytes 4784128 | tf_op jit(solution)/shard_map/srh,srk->hk/dot_general | solution.py:11
  212.0 1.8 bitcast_add_fusion
  (52 shorter events, 10.4 us)
Async XLA Ops:
  7.2 1.2 copy-start
  7.2 64.8 %all-gather.8.cloned.1.call-start = ((), (), s32[]{:S(2)}) async-start(), calls=%async_computation.3 | async-start | bytes 2703360 | tf_op jit(solution)/shard_map/all_gather | solution.py:42
  9.8 123.5 %all-gather.10.cloned.1.call-start = ((), (), s32[]{:S(2)}) async-start(), calls=%async_computation.4 | async-start | bytes 4456448 | tf_op jit(solution)/shard_map/all_gather | solution.py:46
  77.9 5.5 %copy-start.2 = (bf16[128,1024]{1,0:T(8,128)(2,1)S(1)}, bf16[128,1024]{1,0:T(8,128)(2,1)}, u32[]{:S(2)}) copy-start(bf16[128,1024]{1,0:T(8,128)(2,1)} %param.17) | copy-start | bytes 786436
  83.6 8.5 %copy-start.4 = (bf16[16,128,128]{2,1,0:T(8,128)(2,1)S(1)}, bf16[16,128,128]{2,1,0:T(8,128)(2,1)}, u32[]{:S(2)}) copy-start(bf16[16,128,128]{2,1,0:T(8,128)(2,1)} %gather_fusion.1) | copy-start | bytes 1572868
  90.1 2.0 copy-start.1
  92.0 6.7 %copy-start.3 = (f32[128,1024]{1,0:T(8,128)S(1)}, f32[128,1024]{1,0:T(8,128)}, u32[]{:S(2)}) copy-start(f32[128,1024]{1,0:T(8,128)} %convert_element_type.82) | copy-start | bytes 1572868
  94.4 28.2 %all-to-all-start = ((bf16[16,1,129,128]{3,2,1,0:T(8,128)(2,1)}), bf16[16,1,129,128]{3,2,1,0:T(8,128)(2,1)S(1)}, u32[]{:S(2)}, u32[]{:S(2)}) async-start(bf16[16,1,129,128]{3,2,1,0:T(8,128)(2,1)} %maximum_bitcast_fusion), calls=%async_computation | async-start | bytes 1114112 | tf_op jit(solution)/shard_map/all_to_all | solution.py:68
  136.4 14.4 %copy-start.6 = (bf16[512]{0:T(512)(128)(2,1)S(1)}, bf16[512]{0:T(512)(128)(2,1)}, u32[]{:S(2)}) copy-start(bf16[512]{0:T(512)(128)(2,1)} %param.16) | copy-start | bytes 3076
  140.0 9.5 %all-to-all-start.1 = ((bf16[2,1,129,512]{3,2,1,0:T(8,128)(2,1)}), bf16[2,1,129,512]{3,2,1,0:T(8,128)(2,1)S(1)}, u32[]{:S(2)}, u32[]{:S(2)}) async-start(bf16[2,1,129,512]{3,2,1,0:T(8,128)(2,1)} %maximum_bitcast_fusion.1), calls=%async_computation.1 | async-start | bytes 557056 | tf_op jit(solution)/shard_map/all_to_all | solution.py:80
  143.4 48.3 %all-gather.6.cloned.1.call-start = ((), (), s32[]{:S(2)}) async-start(), calls=%async_computation.2 | async-start | bytes 2367488 | tf_op jit(solution)/shard_map/all_gather | solution.py:93
  192.7 4.5 %copy-start.5 = (f32[16,1024]{1,0:T(8,128)S(1)}, f32[16,1024]{1,0:T(8,128)}, u32[]{:S(2)}) copy-start(f32[16,1024]{1,0:T(8,128)} %get-tuple-element.13) | copy-start | bytes 196612
  197.1 12.5 %copy-start.7 = (bf16[16,129,512]{2,1,0:T(8,128)(2,1)S(1)}, bf16[16,129,512]{2,1,0:T(8,128)(2,1)}, u32[]{:S(2)}) copy-start(bf16[16,129,512]{2,1,0:T(8,128)(2,1)} %all-gather.6.cloned.1.call-done) | copy-start | bytes 6340612
Sparse Core Ops, SparseCore 0:
  11.5 60.5 all-gather.7
  74.2 59.0 all-gather.9
  151.7 40.0 all-gather.5
